TPU v7x, 256 devices: a whole 4x4x8 slice. The times are simulated.
256 devices in a mesh: chain: 128 (over y, z, x), grp: 2 (over core).
Axes of the slice: x: 4, y: 4, z: 8, core: 2. Of those that a mesh axis runs over, the one named last changes fastest.
Arguments:
- codes: bfloat16 [2, 16384, 6144], P(None, ('chain', 'grp')), may hold values from -6 to 6
- exponents: int32 [2, 512, 6144], P(None, ('chain', 'grp')), may hold values from -2 to 2
- column_map: int32 [256], replicated, may hold values from 0 to 255, each once
- row_order: int32 [256], replicated, may hold values from 0 to 255, each once
Outputs:
- rollout: bfloat16 [2, 6144, 16384], P(None, ('chain', 'grp'))
- block_sums: float32 [2, 6144, 512], P(None, ('chain', 'grp'))
All inputs are finite; a program needn't handle non-finite values.
Results may differ from a plain program's by a relative error of at most 0.001.
Values may be sent and summed in bfloat16 or wider, within the bound.
A program may use at most 64 MiB of HBM per device.

v0:
```python
import jax
import jax.numpy as jnp
from jax import lax
from jax.sharding import PartitionSpec as P


def cut_along(shard, dim, count):
    before, after = (shard.shape[:dim], shard.shape[dim + 1 :])
    return jnp.moveaxis(shard.reshape(*before, count, -1, *after), dim, 0)


def laid_out(tiles, dim):
    lengths = list(tiles.shape[1:])
    lengths[dim] *= tiles.shape[0]
    return jnp.moveaxis(tiles, 0, dim).reshape(lengths)


def one_exchange(shard, axis, axes, splits, concats):
    sizes = [lax.axis_size(a) for a in axes]
    tiles = cut_along(shard, splits[0], sizes[0])
    tiles = jnp.moveaxis(cut_along(tiles, splits[1] + 1, sizes[1]), 0, 1)
    inside = tiles.shape[2:]
    tiles = tiles.reshape(-1, *inside)
    tiles = lax.all_to_all(tiles, axis, split_axis=0, concat_axis=0, tiled=True)
    tiles = laid_out(tiles.reshape(*sizes, *inside), concats[0] + 1)
    return laid_out(tiles, concats[1])


def arrange(array, column_map, devices, col_width):
    layer_count, row_count, _ = array.shape
    order = (
        jnp.arange(col_width, dtype=jnp.int32)[:, None] + column_map[None, :] * col_width
    ).reshape(-1)
    picked = jnp.take(array, order, axis=2)
    return jnp.swapaxes(picked, 1, 2).reshape(layer_count, col_width, devices, row_count)


def shards(codes, exponents, column_map, row_order):
    chain_size = lax.axis_size("chain")
    grp_size = lax.axis_size("grp")
    devices = chain_size * grp_size
    layer_count, row_count, width_all = codes.shape
    col_width = width_all // devices
    scaling = jnp.exp2(exponents.astype(jnp.float32))
    values = (codes.astype(jnp.float32) * jnp.repeat(scaling, 32, axis=1)).astype(jnp.bfloat16)
    outgoing = arrange(values, column_map, devices, col_width)
    width = outgoing.shape[3]
    shaped = outgoing.reshape(layer_count, col_width, chain_size, grp_size, width)
    arrived = one_exchange(shaped, ("chain", "grp"), ("chain", "grp"), (2, 3), (2, 3))
    arrived = arrived.reshape(layer_count, col_width, devices, width)
    values = arrived
    values = jnp.take(values, row_order, axis=2)
    rollout = values.reshape(layer_count, col_width, devices * row_count)
    block_sums = (
        rollout.astype(jnp.float32)
        .reshape(layer_count, col_width, devices * row_count // 32, 32)
        .sum(axis=-1)
    )
    return (rollout, block_sums)


def solution(mesh):
    return jax.shard_map(
        shards,
        mesh=mesh,
        in_specs=(P(None, ("chain", "grp"), None), P(None, ("chain", "grp"), None), P(), P()),
        out_specs=(P(None, ("chain", "grp"), None), P(None, ("chain", "grp"), None)),
        check_vma=False,
    )
```

profile of v0, /device:TPU:1, one launch (start us, length us, event | category | flops | bytes accessed | tf_op | source)
XLA Modules:
  0.0 170.3 jit_solution(11300951493045494578)
XLA Ops:
  0.6 0.7 broadcast_multiply_fusion
  1.4 1.0 multiply_exponential_fusion
  2.4 2.9 %fusion = bf16[2,64,6144]{2,1,0:T(8,128)(2,1)} fusion(bf16[2,64,6144]{2,1,0:T(8,128)(2,1)} %param.4, f32[2,2,6144]{2,1,0:T(2,128)S(1)} %multiply_exponential_fusion), kind=kLoop, calls=%fused_computation.5 | loop fusion | flops 2359296 | bytes 3244032 | tf_op jit(solution)/shard_map/convert_element_type | solution.py:45
  5.3 6.8 %copy.28 = bf16[2,64,6144]{1,0,2:T(2,128)(2,1)S(1)} copy(bf16[2,64,6144]{2,1,0:T(8,128)(2,1)} %fusion) | data formatting | bytes 3145728 | tf_op jit(solution)/shard_map/convert_element_type | solution.py:45
  12.1 40.4 %gather_fusion = bf16[6144,2,64]{2,1,0:T(2,128)(2,1)} fusion(bf16[2,64,6144]{1,0,2:T(2,128)(2,1)S(1)} %copy.28, s32[6144]{0:T(1024)S(1)} %broadcast_clamp_fusion), kind=kCustom, calls=%fused_computation | custom fusion | bytes 3170304 | tf_op jit(solution)/shard_map/jit(_take)/gather | solution.py:34
  52.6 23.2 %fusion.1 = bf16[2,6144,64]{2,0,1:T(2,128)(2,1)S(1)} fusion(bf16[6144,2,64]{2,1,0:T(2,128)(2,1)} %gather_fusion, pred[6144]{0:T(1024)(128)(4,1)S(1)} %compare_and_fusion), kind=kLoop, calls=%fused_computation.6 | loop fusion | flops 786432 | bytes 3151872 | tf_op jit(solution)/shard_map/jit(_take)/select_n | solution.py:34
  75.8 0.4 copy.29
  76.2 2.0 %copy.40 = bf16[256,2,24,1,1,64]{5,2,1,4,3,0:T(8,128)(2,1)S(1)} copy(bf16[256,2,24,1,1,64]{5,0,2,1,4,3:T(8,128)(2,1)S(1)} %bitcast.41) | data formatting | bytes 3145728 | tf_op jit(solution)/shard_map/reshape | solution.py:23
  78.2 0.0 copy-start.1
  78.2 3.0 %reshape.95 = bf16[256,2,1536]{2,1,0:T(2,128)(2,1)} reshape(bf16[256,1,1,2,24,64]{5,4,3,2,1,0:T(8,128)(2,1)S(1)} %bitcast.42) | data formatting | bytes 3145728
  81.2 16.5 %all-to-all-start = ((bf16[256,2,1536]{2,1,0:T(2,128)(2,1)}), bf16[256,2,1536]{2,1,0:T(2,128)(2,1)}, u32[]{:S(2)}, u32[]{:S(2)}) async-start(bf16[256,2,1536]{2,1,0:T(2,128)(2,1)} %reshape.95), calls=%async_computation | async-start | bytes 3145728 | tf_op jit(solution)/shard_map/all_to_all | solution.py:24
  97.8 0.0 copy-done.1
  97.8 0.1 broadcast_in_dim.47
  97.9 0.2 broadcast_in_dim.48
  98.0 0.1 broadcast_in_dim.39
  98.1 0.1 broadcast_in_dim.40
  98.3 40.9 %all-to-all-done = bf16[256,2,1536]{2,1,0:T(2,128)(2,1)} async-done(((bf16[256,2,1536]{2,1,0:T(2,128)(2,1)}), bf16[256,2,1536]{2,1,0:T(2,128)(2,1)}, u32[]{:S(2)}, u32[]{:S(2)}) %all-to-all-start) | async-done | bytes 1572896 | tf_op jit(solution)/shard_map/all_to_all | solution.py:24
  139.2 4.9 %reshape.96 = bf16[256,1,1,2,24,64]{5,4,3,2,1,0:T(8,128)(2,1)S(1)} reshape(bf16[256,2,1536]{2,1,0:T(2,128)(2,1)} %all-to-all-done) | data formatting | bytes 3145728
  144.1 2.2 %copy.32 = bf16[2,24,128,2,1,64]{5,1,3,2,0,4:T(8,128)(2,1)} copy(bf16[2,24,128,2,1,64]{5,1,0,3,2,4:T(8,128)(2,1)S(1)} %bitcast.43) | data formatting | bytes 3145728 | tf_op jit(solution)/shard_map/transpose | solution.py:15
  146.3 4.7 %gather_fusion.1 = bf16[256,2,24,64]{3,2,1,0:T(8,128)(2,1)} fusion(bf16[2,24,256,64]{3,1,2,0:T(8,128)(2,1)} %bitcast.44, s32[1024]{0:T(1024)S(1)} %pad_clamp_fusion), kind=kCustom, calls=%fused_computation.1 | custom fusion | bytes 3146752 | tf_op jit(solution)/shard_map/jit(_take)/gather | solution.py:52
  151.0 2.7 %copy.33 = bf16[2,24,256,64]{3,2,1,0:T(8,128)(2,1)S(1)} copy(bf16[2,24,256,64]{3,1,0,2:T(8,128)(2,1)} %bitcast.45) | data formatting | bytes 3145728 | tf_op jit(solution)/shard_map/jit(_take)/gather | solution.py:52
  153.7 5.4 %gather.15 = bf16[2,24,512,32]{3,2,1,0:T(8,128)(2,1)} reshape(bf16[2,24,256,64]{3,2,1,0:T(8,128)(2,1)S(1)} %copy.33) | data formatting | bytes 3145728 | tf_op jit(solution)/shard_map/jit(_take)/gather | solution.py:52
  159.0 3.3 %gather.14 = bf16[2,24,16384]{2,1,0:T(8,128)(2,1)} reshape(bf16[2,24,256,64]{3,2,1,0:T(8,128)(2,1)S(1)} %copy.33) | data formatting | bytes 3145728 | tf_op jit(solution)/shard_map/jit(_take)/gather | solution.py:52
  162.3 0.0 copy-start
  162.4 6.6 %convert_reduce_fusion = f32[2,24,512]{2,1,0:T(8,128)} fusion(bf16[2,24,512,32]{3,2,1,0:T(8,128)(2,1)} %gather.15, pred[512]{0:T(512)(128)(4,1)S(1)} %broadcast_in_dim.48), kind=kLoop, calls=%fused_computation.2 | loop fusion | flops 2334720 | bytes 1671680 | tf_op jit(solution)/shard_map/reduce_sum | solution.py:57
  168.9 0.0 copy-done
  168.9 1.4 broadcast_select_fusion.1
  (9 shorter events, 0.1 us)
Async XLA Ops:
  78.2 19.6 %copy-start.1 = (s32[256]{0:T(256)S(1)}, s32[256]{0:T(256)}, u32[]{:S(2)}) copy-start(s32[256]{0:T(256)} %param.7) | copy-start | bytes 3076
  81.2 57.9 %all-to-all-start = ((bf16[256,2,1536]{2,1,0:T(2,128)(2,1)}), bf16[256,2,1536]{2,1,0:T(2,128)(2,1)}, u32[]{:S(2)}, u32[]{:S(2)}) async-start(bf16[256,2,1536]{2,1,0:T(2,128)(2,1)} %reshape.95), calls=%async_computation | async-start | bytes 3145728 | tf_op jit(solution)/shard_map/all_to_all | solution.py:24
  162.3 6.6 %copy-start = (bf16[2,24,16384]{2,1,0:T(8,128)(2,1)S(1)}, bf16[2,24,16384]{2,1,0:T(8,128)(2,1)}, u32[]{:S(2)}) copy-start(bf16[2,24,16384]{2,1,0:T(8,128)(2,1)} %gather.14) | copy-start | bytes 4718596
where the time goes:
time: 171 us; the launch traced here: 170 us
  local copies, waits for them, and re-layouts  76.4 us (45%)
  waiting for transfers between devices  40.9 us (24%)
  other arithmetic  35.7 us (21%)
  starting transfers between devices  16.5 us (10%)
    all_to_all x1, waiting for transfers between devices, one_exchange(): tiles = lax.all_to_all(tiles, axis, split_axis=0, concat_axis=0, tiled=True)  40.9 us
    gather x1, local copies, waits for them, and re-layouts, arrange(): picked = jnp.take(array, order, axis=2)  40.4 us
    select_n x2, other arithmetic, arrange(): picked = jnp.take(array, order, axis=2)  23.2 us
    all_to_all x1, starting transfers between devices, one_exchange(): tiles = lax.all_to_all(tiles, axis, split_axis=0, concat_axis=0, tiled=True)  16.5 us
    gather x4, local copies, waits for them, and re-layouts, shards(): values = jnp.take(values, row_order, axis=2)  16.1 us
    unnamed x8, local copies, waits for them, and re-layouts  7.97 us
    convert_element_type x1, local copies, waits for them, and re-layouts, shards(): (codes.astype(jnp.float32) * jnp.repeat(scaling, 32, axis=1)).astype(jnp....  6.84 us
    reduce_sum x1, other arithmetic, shards(): block_sums = rollout.astype(jnp.float32).reshape(layer_count, col_width,...  6.57 us
  transfers between devices with their start and end apart: 1, of which 1 were waited for; matrix products, arithmetic and copies ran while one was open for 0% of the time, Pallas kernels for 0%

commit v1 on v0

v1 whole, which is shorter than its diff:
```python
import functools

import jax
import jax.numpy as jnp
from jax import lax
from jax.experimental import pallas as pl
from jax.experimental.pallas import tpu as pltpu
from jax.sharding import PartitionSpec as P

MESH = pl.DeviceIdType.MESH
BLOCK = 32
LANES = 128


def exchange(sizes, codes_hbm, exps_hbm, cmap_hbm, recv, codes, exps, cmap, turned, send, load_sem, own_sem, send_sem, recv_sem):
    x_size, y_size, z_size, g_size = sizes
    devices = x_size * y_size * z_size * g_size
    layers, rows, width = codes.shape
    col_width = width // devices
    chain, g = lax.axis_index("chain"), lax.axis_index("grp")
    x, z, y = chain % x_size, (chain // x_size) % z_size, chain // (x_size * z_size)
    me = chain * g_size + g

    loads = [
        pltpu.make_async_copy(codes_hbm, codes, load_sem.at[0]),
        pltpu.make_async_copy(exps_hbm, exps, load_sem.at[1]),
        pltpu.make_async_copy(cmap_hbm, cmap, load_sem.at[2]),
    ]
    for load in loads:
        load.start()

    def peer(step):
        dz, dx = step % z_size, (step // z_size) % x_size
        dy, dg = (step // (z_size * x_size)) % y_size, step // (z_size * x_size * y_size)
        to = (((y + dy) % y_size) * z_size + (z + dz) % z_size) * x_size + (x + dx) % x_size
        return to, (g + dg) % g_size

    barrier = pltpu.get_barrier_semaphore()

    @pl.loop(1, devices)
    def _(step):
        pl.semaphore_signal(barrier, inc=1, device_id=peer(step), device_id_type=MESH)

    for load in loads:
        load.wait()

    group = LANES // 8
    span = group * col_width

    @pl.loop(0, width // span)
    def _(chunk):
        lanes = pl.ds(pl.multiple_of(chunk * span, LANES), span)
        parts = []
        for layer in range(layers):
            for block in range(rows // BLOCK):
                scale = jnp.exp2(exps[layer, block : block + 1, lanes].astype(jnp.float32))
                value = codes[layer, block * BLOCK : (block + 1) * BLOCK, lanes].astype(jnp.float32)
                parts.append(value * scale)
        blocks = jnp.concatenate(parts, axis=0).T.reshape(group, col_width, layers * rows)
        turned[pl.ds(chunk * group, group)] = blocks

    @pl.loop(0, devices)
    def _(to):
        send[to] = turned[cmap[to]].astype(send.dtype)

    pl.semaphore_wait(barrier, devices - 1)

    @pl.loop(1, devices)
    def _(step):
        to, to_g = peer(step)
        pltpu.make_async_remote_copy(
            src_ref=send.at[to * g_size + to_g],
            dst_ref=recv.at[me],
            send_sem=send_sem,
            recv_sem=recv_sem,
            device_id=(to, to_g),
            device_id_type=MESH,
        ).start()

    own = pltpu.make_async_copy(send.at[me], recv.at[me], own_sem)
    own.start()
    own.wait()
    others = pl.ds(0, devices - 1)
    pltpu.make_async_copy(recv.at[others], recv.at[others], recv_sem).wait()
    pltpu.make_async_copy(send.at[others], send.at[others], send_sem).wait()


def assemble(order, recv, rollout, sums):
    layers, col_width, span = rollout.shape
    half = LANES // layers
    first = pl.program_id(0) * (span // half)
    low = lax.broadcasted_iota(jnp.int32, (col_width, LANES), 1) < half
    group = 2 * LANES
    totals = [jnp.zeros((col_width, LANES), jnp.float32) for _ in range(layers)]
    row = lax.broadcasted_iota(jnp.int32, (group, LANES), 0) // BLOCK
    lane = lax.broadcasted_iota(jnp.int32, (group, LANES), 1)
    for at in range(0, span, group):
        tiles = [[] for _ in range(layers)]
        for pair in range(at, at + group, LANES):
            k = first + pair // half
            a, b = recv[order[k]], recv[order[k + 1]]
            tiles[0].append(jnp.concatenate([a[:, :half], b[:, :half]], axis=1))
            tiles[1].append(jnp.concatenate([a[:, half:], b[:, half:]], axis=1))
        picks = (row + at // BLOCK == lane).astype(jnp.bfloat16)
        for layer in range(layers):
            both = jnp.concatenate(tiles[layer], axis=1)
            rollout[layer, :, at : at + group] = both
            totals[layer] += jnp.dot(both, picks, preferred_element_type=jnp.float32)
    for layer in range(layers):
        sums[layer] = totals[layer]


def shards(sizes, codes, exponents, column_map, row_order):
    layers, rows, width = codes.shape
    devices = sizes[0] * sizes[1] * sizes[2] * sizes[3]
    col_width = width // devices
    anywhere = pl.BlockSpec(memory_space=pl.ANY)
    landed = pl.pallas_call(
        functools.partial(exchange, sizes),
        out_shape=jax.ShapeDtypeStruct((devices, col_width, layers * rows), jnp.bfloat16),
        in_specs=[anywhere] * 3,
        out_specs=anywhere,
        scratch_shapes=[
            pltpu.VMEM(codes.shape, codes.dtype),
            pltpu.VMEM(exponents.shape, exponents.dtype),
            pltpu.SMEM(column_map.shape, column_map.dtype),
            pltpu.VMEM((devices, col_width, layers * rows), jnp.float32),
            pltpu.VMEM((devices, col_width, layers * rows), jnp.bfloat16),
            pltpu.SemaphoreType.DMA((3,)),
            pltpu.SemaphoreType.DMA(()),
            pltpu.SemaphoreType.DMA(()),
            pltpu.SemaphoreType.DMA(()),
        ],
        compiler_params=pltpu.CompilerParams(
            collective_id=0, has_side_effects=True, vmem_limit_bytes=16 << 20
        ),
        name="exchange",
    )(codes, exponents, column_map)
    span = LANES * BLOCK
    return pl.pallas_call(
        assemble,
        grid=(devices * rows // span,),
        out_shape=(
            jax.ShapeDtypeStruct((layers, col_width, devices * rows), jnp.bfloat16),
            jax.ShapeDtypeStruct((layers, col_width, devices * rows // BLOCK), jnp.float32),
        ),
        in_specs=[
            pl.BlockSpec(memory_space=pltpu.SMEM),
            pl.BlockSpec(memory_space=pltpu.VMEM),
        ],
        out_specs=(
            pl.BlockSpec((layers, col_width, span), lambda i: (0, 0, i)),
            pl.BlockSpec((layers, col_width, LANES), lambda i: (0, 0, i)),
        ),
        compiler_params=pltpu.CompilerParams(vmem_limit_bytes=16 << 20),
        name="assemble",
    )(row_order, landed)


def solution(mesh):
    chain, grp = mesh.shape["chain"], mesh.shape["grp"]
    z_size = next(n for n in range(1, chain + 1) if n ** 3 >= 4 * chain)
    side = 1
    while side * side * z_size < chain:
        side += 1
    sizes = (side, side, z_size, grp)
    assert side * side * z_size == chain
    return jax.shard_map(
        functools.partial(shards, sizes),
        mesh=mesh,
        in_specs=(P(None, ("chain", "grp"), None), P(None, ("chain", "grp"), None), P(), P()),
        out_specs=(P(None, ("chain", "grp"), None), P(None, ("chain", "grp"), None)),
        check_vma=False,
    )
```

time: 171 us -> 66.5 us (0.39)
  local copies, waits for them, and re-layouts: 76.4 us -> 2.98 us
  Pallas kernels: 0 us -> 62.7 us
  waiting for transfers between devices: 40.9 us -> 0 us
  other arithmetic: 35.7 us -> 0 us
  starting transfers between devices: 16.5 us -> 0 us
    pallas_call x0 -> x2, Pallas kernels: none -> 62.7 us  [the longest x1 59.4 us: shards(): pl.pallas_call(functools.partial(exchange, sizes), out_shape=jax.ShapeDty...]
    gather x5 -> x0, local copies, waits for them, and re-layouts: 56.5 us -> none  [the longest x1 40.4 us: arrange(): picked = jnp.take(array, order, axis=2)]
    all_to_all x1 -> x0, waiting for transfers between devices: 40.9 us -> none  [one_exchange(): tiles = lax.all_to_all(tiles, axis, split_axis=0, concat_axis=0, tiled=True)]
    select_n x4 -> x0, other arithmetic: 24.6 us -> none  [the longest x2 23.2 us: arrange(): picked = jnp.take(array, order, axis=2)]
    all_to_all x1 -> x0, starting transfers between devices: 16.5 us -> none  [one_exchange(): tiles = lax.all_to_all(tiles, axis, split_axis=0, concat_axis=0, tiled=True)]
    convert_element_type x1 -> x0, local copies, waits for them, and re-layouts: 6.84 us -> none  [shards(): (codes.astype(jnp.float32) * jnp.repeat(scaling, 32, axis=1)).astype(jnp....]
    reduce_sum x1 -> x0, other arithmetic: 6.57 us -> none  [shards(): block_sums = rollout.astype(jnp.float32).reshape(layer_count, col_width,...]
    unnamed x8, local copies, waits for them, and re-layouts: 7.97 us -> 2.98 us
  transfers between devices with their start and end apart: 1 -> 0, of which waited for: 1 -> 0; matrix products, arithmetic and copies ran while one was open for 0% -> 0% of each run, Pallas kernels for 0% -> 0%
where the time goes in v1:
time: 66.5 us; the launch traced here: 66.3 us
  Pallas kernels  62.7 us (94%)
  local copies, waits for them, and re-layouts  2.98 us (4%)
    pallas_call x1, Pallas kernels, shards(): pl.pallas_call(functools.partial(exchange, sizes), out_shape=jax.ShapeDty...  59.4 us
    pallas_call x1, Pallas kernels, shards(): pl.pallas_call(assemble, grid=(devices * rows // span,), out_shape=(jax.S...  3.33 us
    unnamed x8, local copies, waits for them, and re-layouts  2.98 us

profile of v1, /device:TPU:1, one launch (start us, length us, event | category | flops | bytes accessed | tf_op | source)
XLA Modules:
  0.0 66.3 jit_solution(14801933776035926782)
XLA Ops:
  0.6 0.0 copy-start
  0.6 1.4 %copy-done = bf16[2,64,6144]{2,1,0:T(8,128)(2,1)S(1)} copy-done((bf16[2,64,6144]{2,1,0:T(8,128)(2,1)S(1)}, bf16[2,64,6144]{2,1,0:T(8,128)(2,1)}, u32[]{:S(2)}) %copy-start) | copy-done | bytes 1572888
  2.0 0.0 copy-start.1
  2.0 0.9 %copy-done.1 = s32[2,2,6144]{2,1,0:T(2,128)S(1)} copy-done((s32[2,2,6144]{2,1,0:T(2,128)S(1)}, s32[2,2,6144]{2,1,0:T(2,128)}, u32[]{:S(2)}) %copy-start.1) | copy-done | bytes 98328
  2.9 0.0 copy-start.2
  2.9 0.7 %copy-done.2 = s32[256]{0:T(256)S(1)} copy-done((s32[256]{0:T(256)S(1)}, s32[256]{0:T(256)}, u32[]{:S(2)}) %copy-start.2) | copy-done | bytes 1048
  3.6 0.0 copy-start.3
  3.6 59.4 %exchange.1.recv = bf16[256,24,128]{2,1,0:T(8,128)(2,1)S(1)} custom-call(bf16[2,64,6144]{2,1,0:T(8,128)(2,1)S(1)} %copy-done, s32[2,2,6144]{2,1,0:T(2,128)S(1)} %copy-done.1, s32[256]{0:T(256)S(1)} %copy-done.2), custom_call_target="tpu_custom_call" | custom-call | tf_op jit(solution)/shard_map/exchange/pallas_call | solution.py:118
  63.0 0.0 copy-done.3
  63.0 3.3 %assemble.1 = (bf16[2,24,16384]{2,1,0:T(8,128)(2,1)}, f32[2,24,512]{2,1,0:T(8,128)}) custom-call(s32[256]{0:T(256)S(1)} %copy-done.3, bf16[256,24,128]{2,1,0:T(8,128)(2,1)S(1)} %exchange.1.recv), custom_call_target="tpu_custom_call" | custom-call | tf_op jit(solution)/shard_map/assemble/pallas_call | solution.py:140
Async XLA Ops:
  0.6 1.4 %copy-start = (bf16[2,64,6144]{2,1,0:T(8,128)(2,1)S(1)}, bf16[2,64,6144]{2,1,0:T(8,128)(2,1)}, u32[]{:S(2)}) copy-start(bf16[2,64,6144]{2,1,0:T(8,128)(2,1)} %codes_hbm.1) | copy-start | bytes 4718596
  2.0 0.9 %copy-start.1 = (s32[2,2,6144]{2,1,0:T(2,128)S(1)}, s32[2,2,6144]{2,1,0:T(2,128)}, u32[]{:S(2)}) copy-start(s32[2,2,6144]{2,1,0:T(2,128)} %exps_hbm.1) | copy-start | bytes 294916
  2.9 0.7 %copy-start.2 = (s32[256]{0:T(256)S(1)}, s32[256]{0:T(256)}, u32[]{:S(2)}) copy-start(s32[256]{0:T(256)} %cmap_hbm.1) | copy-start | bytes 3076
  3.6 59.4 %copy-start.3 = (s32[256]{0:T(256)S(1)}, s32[256]{0:T(256)}, u32[]{:S(2)}) copy-start(s32[256]{0:T(256)} %order.1) | copy-start | bytes 3076

commit v2 on v1

--- a/solution.py
+++ b/solution.py
@@ -12,14 +12,47 @@
 LANES = 128
 
 
-def exchange(sizes, codes_hbm, exps_hbm, cmap_hbm, recv, codes, exps, cmap, turned, send, load_sem, own_sem, send_sem, recv_sem):
+def hops(d, size):
+    return min(d, size - d)
+
+
+def plan(sizes):
+    x_size, y_size, z_size, g_size = sizes
+
+    def distance(o):
+        return hops(o[0], x_size) + hops(o[1], y_size) + hops(o[2], z_size)
+
+    offsets = [
+        (dx, dy, dz, dg)
+        for dg in range(g_size)
+        for dy in range(y_size)
+        for dx in range(x_size)
+        for dz in range(z_size)
+    ][1:]
+    reach = hops(x_size // 2, x_size) + hops(y_size // 2, y_size)
+    reach = max(reach, hops(z_size // 2, z_size))
+    middles = [(0, 0, z_size // 2, 0), (x_size // 2, y_size // 2, 0, 0)]
+    ordered = []
+    for o in sorted(offsets, key=lambda o: -distance(o)):
+        back = (-o[0] % x_size, -o[1] % y_size, -o[2] % z_size)
+        for twin in (o[:3], back):
+            for dg in range(g_size):
+                if twin + (dg,) in offsets and twin + (dg,) not in ordered:
+                    ordered.append(twin + (dg,))
+    near = [o for o in ordered if distance(o) <= reach]
+    far = [o for o in ordered if distance(o) > reach]
+    for o in far:
+        gaps = [tuple((p - q) % n for p, q, n in zip(o, m, sizes)) for m in middles]
+        assert any(distance(gap) <= reach for gap in gaps)
+    return near, far, [m for m in middles if m in near]
+
+
+def exchange(sizes, codes_hbm, exps_hbm, cmap_hbm, recv, codes, exps, cmap, turned, send, load_sem, send_sem, recv_sem, mid_sem):
     x_size, y_size, z_size, g_size = sizes
     devices = x_size * y_size * z_size * g_size
     layers, rows, width = codes.shape
     col_width = width // devices
-    chain, g = lax.axis_index("chain"), lax.axis_index("grp")
-    x, z, y = chain % x_size, (chain // x_size) % z_size, chain // (x_size * z_size)
-    me = chain * g_size + g
+    near, far, middles = plan(sizes)
 
     loads = [
         pltpu.make_async_copy(codes_hbm, codes, load_sem.at[0]),
@@ -29,17 +62,21 @@
     for load in loads:
         load.start()
 
-    def peer(step):
-        dz, dx = step % z_size, (step // z_size) % x_size
-        dy, dg = (step // (z_size * x_size)) % y_size, step // (z_size * x_size * y_size)
-        to = (((y + dy) % y_size) * z_size + (z + dz) % z_size) * x_size + (x + dx) % x_size
-        return to, (g + dg) % g_size
+    chain, g = lax.axis_index("chain"), lax.axis_index("grp")
+    x, z, y = lax.rem(chain, x_size), lax.rem(lax.div(chain, x_size), z_size), lax.div(chain, x_size * z_size)
+    me = chain * g_size + g
+    across = [lax.rem(x + d, x_size) for d in range(x_size)]
+    along = [lax.rem(z + d, z_size) * x_size for d in range(z_size)]
+    down = [lax.rem(y + d, y_size) * (x_size * z_size) for d in range(y_size)]
+    cores = [lax.rem(g + d, g_size) for d in range(g_size)]
+    planes = {(dx, dy): down[dy] + across[dx] for dx in range(x_size) for dy in range(y_size)}
+
+    def peer(o):
+        return planes[o[:2]] + along[o[2]], cores[o[3]]
 
     barrier = pltpu.get_barrier_semaphore()
-
-    @pl.loop(1, devices)
-    def _(step):
-        pl.semaphore_signal(barrier, inc=1, device_id=peer(step), device_id_type=MESH)
+    for o in near:
+        pl.semaphore_signal(barrier, inc=1, device_id=peer(o), device_id_type=MESH)
 
     for load in loads:
         load.wait()
@@ -59,30 +96,35 @@
         blocks = jnp.concatenate(parts, axis=0).T.reshape(group, col_width, layers * rows)
         turned[pl.ds(chunk * group, group)] = blocks
 
-    @pl.loop(0, devices)
-    def _(to):
-        send[to] = turned[cmap[to]].astype(send.dtype)
-
-    pl.semaphore_wait(barrier, devices - 1)
-
-    @pl.loop(1, devices)
-    def _(step):
-        to, to_g = peer(step)
+    def gather(slot, o):
+        to, to_g = peer(o)
+        send[slot] = turned[cmap[to * g_size + to_g]].astype(send.dtype)
+
+    def launch(slot, o):
         pltpu.make_async_remote_copy(
-            src_ref=send.at[to * g_size + to_g],
+            src_ref=send.at[slot],
             dst_ref=recv.at[me],
             send_sem=send_sem,
             recv_sem=recv_sem,
-            device_id=(to, to_g),
+            device_id=peer(o),
             device_id_type=MESH,
         ).start()
 
-    own = pltpu.make_async_copy(send.at[me], recv.at[me], own_sem)
-    own.start()
-    own.wait()
-    others = pl.ds(0, devices - 1)
-    pltpu.make_async_copy(recv.at[others], recv.at[others], recv_sem).wait()
-    pltpu.make_async_copy(send.at[others], send.at[others], send_sem).wait()
+    recv[me] = turned[cmap[me]].astype(recv.dtype)
+    for slot, o in enumerate(near + far):
+        gather(slot, o)
+
+    pl.semaphore_wait(barrier, len(near))
+    for m in middles:
+        pl.semaphore_signal(mid_sem, inc=1, device_id=peer(m), device_id_type=MESH)
+    for slot, o in enumerate(near):
+        launch(slot, o)
+    pl.semaphore_wait(mid_sem, len(middles))
+    for slot, o in enumerate(far):
+        launch(len(near) + slot, o)
+    others = recv.at[pl.ds(0, devices - 1)]
+    pltpu.make_async_copy(others, others, recv_sem).wait()
+    pltpu.make_async_copy(send, send, send_sem).wait()
 
 
 def assemble(order, recv, rollout, sums):
@@ -117,22 +159,22 @@
     anywhere = pl.BlockSpec(memory_space=pl.ANY)
     landed = pl.pallas_call(
         functools.partial(exchange, sizes),
-        out_shape=jax.ShapeDtypeStruct((devices, col_width, layers * rows), jnp.bfloat16),
+        out_shape=pltpu.VMEM((devices, col_width, layers * rows), jnp.bfloat16),
         in_specs=[anywhere] * 3,
-        out_specs=anywhere,
+        out_specs=pl.BlockSpec(memory_space=pltpu.VMEM),
         scratch_shapes=[
             pltpu.VMEM(codes.shape, codes.dtype),
             pltpu.VMEM(exponents.shape, exponents.dtype),
             pltpu.SMEM(column_map.shape, column_map.dtype),
             pltpu.VMEM((devices, col_width, layers * rows), jnp.float32),
-            pltpu.VMEM((devices, col_width, layers * rows), jnp.bfloat16),
+            pltpu.VMEM((devices - 1, col_width, layers * rows), jnp.bfloat16),
             pltpu.SemaphoreType.DMA((3,)),
             pltpu.SemaphoreType.DMA(()),
             pltpu.SemaphoreType.DMA(()),
-            pltpu.SemaphoreType.DMA(()),
+            pltpu.SemaphoreType.REGULAR,
         ],
         compiler_params=pltpu.CompilerParams(
-            collective_id=0, has_side_effects=True, vmem_limit_bytes=16 << 20
+            collective_id=0, has_side_effects=True, vmem_limit_bytes=60 << 20
         ),
         name="exchange",
     )(codes, exponents, column_map)

time: 66.5 us -> 54.2 us (0.82)
  Pallas kernels: 62.7 us -> 53.4 us
  local copies, waits for them, and re-layouts: 2.98 us -> 0.01 us
    pallas_call x1, Pallas kernels: 59.4 us -> 50.1 us  [shards(): pl.pallas_call(functools.partial(exchange, sizes), out_shape=pltpu.VMEM((...]
    unnamed x8 -> x2, local copies, waits for them, and re-layouts: 2.98 us -> 0.01 us
where the time goes in v2:
time: 54.2 us; the launch traced here: 54.1 us
  Pallas kernels  53.4 us (99%)
  between operations  0.65 us (1%)
    pallas_call x1, Pallas kernels, shards(): pl.pallas_call(functools.partial(exchange, sizes), out_shape=pltpu.VMEM((...  50.1 us
    pallas_call x1, Pallas kernels, shards(): pl.pallas_call(assemble, grid=(devices * rows // span,), out_shape=(jax.S...  3.35 us

profile of v2, /device:TPU:1, one launch (start us, length us, event | category | flops | bytes accessed | tf_op | source)
XLA Modules:
  0.0 54.1 jit_solution(3288821376597697623)
XLA Ops:
  0.6 0.0 copy-start
  0.6 50.1 %exchange.1.recv = bf16[256,24,128]{2,1,0:T(8,128)(2,1)S(1)} custom-call(bf16[2,64,6144]{2,1,0:T(8,128)(2,1)} %codes_hbm.1, s32[2,2,6144]{2,1,0:T(2,128)} %exps_hbm.1, s32[256]{0:T(256)} %cmap_hbm.1), custom_call_target="tpu_custom_call" | custom-call | tf_op jit(solution)/shard_map/exchange/pallas_call | solution.py:160
  50.7 0.0 copy-done
  50.8 3.3 %assemble.1 = (bf16[2,24,16384]{2,1,0:T(8,128)(2,1)}, f32[2,24,512]{2,1,0:T(8,128)}) custom-call(s32[256]{0:T(256)S(1)} %copy-done, bf16[256,24,128]{2,1,0:T(8,128)(2,1)S(1)} %exchange.1.recv), custom_call_target="tpu_custom_call" | custom-call | tf_op jit(solution)/shard_map/assemble/pallas_call | solution.py:182
Async XLA Ops:
  0.6 50.1 %copy-start = (s32[256]{0:T(256)S(1)}, s32[256]{0:T(256)}, u32[]{:S(2)}) copy-start(s32[256]{0:T(256)} %order.1) | copy-start | bytes 3076

commit v3 on v2

--- a/solution.py
+++ b/solution.py
@@ -54,13 +54,17 @@
     col_width = width // devices
     near, far, middles = plan(sizes)
 
-    loads = [
-        pltpu.make_async_copy(codes_hbm, codes, load_sem.at[0]),
-        pltpu.make_async_copy(exps_hbm, exps, load_sem.at[1]),
-        pltpu.make_async_copy(cmap_hbm, cmap, load_sem.at[2]),
-    ]
-    for load in loads:
-        load.start()
+    pieces = 2
+    piece = width // pieces
+    load_exps = pltpu.make_async_copy(exps_hbm, exps, load_sem.at[pieces])
+    load_exps.start()
+    loads = []
+    for i in range(pieces):
+        lanes = pl.ds(i * piece, piece)
+        loads.append(pltpu.make_async_copy(codes_hbm.at[:, :, lanes], codes.at[:, :, lanes], load_sem.at[i]))
+        loads[-1].start()
+    load_cmap = pltpu.make_async_copy(cmap_hbm, cmap, load_sem.at[pieces + 1])
+    load_cmap.start()
 
     chain, g = lax.axis_index("chain"), lax.axis_index("grp")
     x, z, y = lax.rem(chain, x_size), lax.rem(lax.div(chain, x_size), z_size), lax.div(chain, x_size * z_size)
@@ -78,27 +82,26 @@
     for o in near:
         pl.semaphore_signal(barrier, inc=1, device_id=peer(o), device_id_type=MESH)
 
-    for load in loads:
-        load.wait()
-
+    load_exps.wait()
     group = LANES // 8
     span = group * col_width
-
-    @pl.loop(0, width // span)
-    def _(chunk):
-        lanes = pl.ds(pl.multiple_of(chunk * span, LANES), span)
+    for chunk in range(width // span):
+        if chunk * span % piece == 0:
+            loads[chunk * span // piece].wait()
+        lanes = pl.ds(chunk * span, span)
         parts = []
         for layer in range(layers):
             for block in range(rows // BLOCK):
                 scale = jnp.exp2(exps[layer, block : block + 1, lanes].astype(jnp.float32))
-                value = codes[layer, block * BLOCK : (block + 1) * BLOCK, lanes].astype(jnp.float32)
-                parts.append(value * scale)
+                part = codes[layer, block * BLOCK : (block + 1) * BLOCK, lanes]
+                parts.append(part * scale.astype(part.dtype))
         blocks = jnp.concatenate(parts, axis=0).T.reshape(group, col_width, layers * rows)
         turned[pl.ds(chunk * group, group)] = blocks
+    load_cmap.wait()
 
     def gather(slot, o):
         to, to_g = peer(o)
-        send[slot] = turned[cmap[to * g_size + to_g]].astype(send.dtype)
+        send[slot] = turned[cmap[to * g_size + to_g]]
 
     def launch(slot, o):
         pltpu.make_async_remote_copy(
@@ -110,7 +113,7 @@
             device_id_type=MESH,
         ).start()
 
-    recv[me] = turned[cmap[me]].astype(recv.dtype)
+    recv[me] = turned[cmap[me]]
     for slot, o in enumerate(near + far):
         gather(slot, o)
 
@@ -127,29 +130,44 @@
     pltpu.make_async_copy(send, send, send_sem).wait()
 
 
-def assemble(order, recv, rollout, sums):
-    layers, col_width, span = rollout.shape
+def assemble(order, recv, rollout, sums, tiles, totals, out_sem):
+    layers, col_width, width = rollout.shape
     half = LANES // layers
-    first = pl.program_id(0) * (span // half)
-    low = lax.broadcasted_iota(jnp.int32, (col_width, LANES), 1) < half
-    group = 2 * LANES
-    totals = [jnp.zeros((col_width, LANES), jnp.float32) for _ in range(layers)]
-    row = lax.broadcasted_iota(jnp.int32, (group, LANES), 0) // BLOCK
-    lane = lax.broadcasted_iota(jnp.int32, (group, LANES), 1)
-    for at in range(0, span, group):
-        tiles = [[] for _ in range(layers)]
-        for pair in range(at, at + group, LANES):
-            k = first + pair // half
-            a, b = recv[order[k]], recv[order[k + 1]]
-            tiles[0].append(jnp.concatenate([a[:, :half], b[:, :half]], axis=1))
-            tiles[1].append(jnp.concatenate([a[:, half:], b[:, half:]], axis=1))
-        picks = (row + at // BLOCK == lane).astype(jnp.bfloat16)
+    quad = 2 * LANES
+    span = LANES * BLOCK
+    part = span // 2
+    lane = lax.broadcasted_iota(jnp.int32, (col_width, LANES), 1)
+    low = lane < half
+    sources = lax.broadcasted_iota(jnp.int32, (quad, LANES), 0) // BLOCK
+    targets = lax.broadcasted_iota(jnp.int32, (quad, LANES), 1) % (quad // BLOCK)
+    picks = (sources == targets).astype(jnp.bfloat16)
+    copies = []
+    for at in range(0, width, LANES):
+        k = at // half
+        a, b = recv[order[k]], recv[order[k + 1]]
+        crossed = pltpu.roll(jnp.where(low, b, a), half, 1)
+        tiles[0, :, at : at + LANES] = jnp.where(low, a, crossed)
+        tiles[1, :, at : at + LANES] = jnp.where(low, crossed, b)
+        done = at + LANES
+        if done % part == 0:
+            lanes = pl.ds(done - part, part)
+            copies.append(pltpu.make_async_copy(tiles.at[:, :, lanes], rollout.at[:, :, lanes], out_sem.at[done // part - 1]))
+            copies[-1].start()
+    for start in range(0, width, span):
         for layer in range(layers):
-            both = jnp.concatenate(tiles[layer], axis=1)
-            rollout[layer, :, at : at + group] = both
-            totals[layer] += jnp.dot(both, picks, preferred_element_type=jnp.float32)
-    for layer in range(layers):
-        sums[layer] = totals[layer]
+            stacked = jnp.concatenate(
+                [tiles[layer, :, at : at + quad] for at in range(start, start + span, quad)], axis=0
+            )
+            got = jnp.dot(stacked, picks, preferred_element_type=jnp.float32)
+            got = got.reshape(span // quad, col_width, LANES)
+            total = got[0]
+            for i in range(1, span // quad):
+                total = jnp.where(lane // (quad // BLOCK) == i, got[i], total)
+            totals[layer, :, start // BLOCK : start // BLOCK + LANES] = total
+    copies.append(pltpu.make_async_copy(totals, sums, out_sem.at[width // part]))
+    copies[-1].start()
+    for copy in copies:
+        copy.wait()
 
 
 def shards(sizes, codes, exponents, column_map, row_order):
@@ -166,9 +184,9 @@
             pltpu.VMEM(codes.shape, codes.dtype),
             pltpu.VMEM(exponents.shape, exponents.dtype),
             pltpu.SMEM(column_map.shape, column_map.dtype),
-            pltpu.VMEM((devices, col_width, layers * rows), jnp.float32),
+            pltpu.VMEM((devices, col_width, layers * rows), codes.dtype),
             pltpu.VMEM((devices - 1, col_width, layers * rows), jnp.bfloat16),
-            pltpu.SemaphoreType.DMA((3,)),
+            pltpu.SemaphoreType.DMA((4,)),
             pltpu.SemaphoreType.DMA(()),
             pltpu.SemaphoreType.DMA(()),
             pltpu.SemaphoreType.REGULAR,
@@ -178,22 +196,21 @@
         ),
         name="exchange",
     )(codes, exponents, column_map)
-    span = LANES * BLOCK
+    rollout = jax.ShapeDtypeStruct((layers, col_width, devices * rows), jnp.bfloat16)
+    sums = jax.ShapeDtypeStruct((layers, col_width, devices * rows // BLOCK), jnp.float32)
     return pl.pallas_call(
         assemble,
-        grid=(devices * rows // span,),
-        out_shape=(
-            jax.ShapeDtypeStruct((layers, col_width, devices * rows), jnp.bfloat16),
-            jax.ShapeDtypeStruct((layers, col_width, devices * rows // BLOCK), jnp.float32),
-        ),
+        out_shape=(rollout, sums),
         in_specs=[
             pl.BlockSpec(memory_space=pltpu.SMEM),
             pl.BlockSpec(memory_space=pltpu.VMEM),
         ],
-        out_specs=(
-            pl.BlockSpec((layers, col_width, span), lambda i: (0, 0, i)),
-            pl.BlockSpec((layers, col_width, LANES), lambda i: (0, 0, i)),
-        ),
+        out_specs=(anywhere, anywhere),
+        scratch_shapes=[
+            pltpu.VMEM(rollout.shape, rollout.dtype),
+            pltpu.VMEM(sums.shape, sums.dtype),
+            pltpu.SemaphoreType.DMA((9,)),
+        ],
         compiler_params=pltpu.CompilerParams(vmem_limit_bytes=16 << 20),
         name="assemble",
     )(row_order, landed)

time: 54.2 us -> 52.8 us (0.974)
  Pallas kernels: 53.4 us -> 52.1 us
    pallas_call x1, Pallas kernels: 3.35 us -> 2.16 us  [shards(): pl.pallas_call(assemble, out_shape=(rollout, sums), in_specs=[pl.BlockSpe...]
where the time goes in v3:
time: 52.8 us
  Pallas kernels  52.1 us (99%)
  between operations  0.65 us (1%)
    pallas_call x1, Pallas kernels, shards(): pl.pallas_call(functools.partial(exchange, sizes), out_shape=pltpu.VMEM((...  49.9 us
    pallas_call x1, Pallas kernels, shards(): pl.pallas_call(assemble, out_shape=(rollout, sums), in_specs=[pl.BlockSpe...  2.16 us

profile of v3, /device:TPU:1, one launch (start us, length us, event | category | flops | bytes accessed | tf_op | source)
XLA Modules:
  0.0 52.8 jit_solution(16236288164063829802)
XLA Ops:
  0.6 0.0 copy-start
  0.6 49.9 %exchange.1.recv = bf16[256,24,128]{2,1,0:T(8,128)(2,1)S(1)} custom-call(bf16[2,64,6144]{2,1,0:T(8,128)(2,1)} %codes_hbm.1, s32[2,2,6144]{2,1,0:T(2,128)} %exps_hbm.1, s32[256]{0:T(256)} %cmap_hbm.1), custom_call_target="tpu_custom_call" | custom-call | tf_op jit(solution)/shard_map/exchange/pallas_call | solution.py:178
  50.6 0.0 copy-done
  50.6 2.2 %assemble.1 = (bf16[2,24,16384]{2,1,0:T(8,128)(2,1)}, f32[2,24,512]{2,1,0:T(8,128)}) custom-call(s32[256]{0:T(256)S(1)} %copy-done, bf16[256,24,128]{2,1,0:T(8,128)(2,1)S(1)} %exchange.1.recv), custom_call_target="tpu_custom_call" | custom-call | tf_op jit(solution)/shard_map/assemble/pallas_call | solution.py:201
Async XLA Ops:
  0.6 50.0 %copy-start = (s32[256]{0:T(256)S(1)}, s32[256]{0:T(256)}, u32[]{:S(2)}) copy-start(s32[256]{0:T(256)} %order.1) | copy-start | bytes 3076

commit v4 on v3

--- a/solution.py
+++ b/solution.py
@@ -18,41 +18,61 @@
 
 def plan(sizes):
     x_size, y_size, z_size, g_size = sizes
-
-    def distance(o):
-        return hops(o[0], x_size) + hops(o[1], y_size) + hops(o[2], z_size)
-
     offsets = [
         (dx, dy, dz, dg)
         for dg in range(g_size)
         for dy in range(y_size)
         for dx in range(x_size)
         for dz in range(z_size)
-    ][1:]
-    reach = hops(x_size // 2, x_size) + hops(y_size // 2, y_size)
-    reach = max(reach, hops(z_size // 2, z_size))
-    middles = [(0, 0, z_size // 2, 0), (x_size // 2, y_size // 2, 0, 0)]
-    ordered = []
-    for o in sorted(offsets, key=lambda o: -distance(o)):
-        back = (-o[0] % x_size, -o[1] % y_size, -o[2] % z_size)
-        for twin in (o[:3], back):
-            for dg in range(g_size):
-                if twin + (dg,) in offsets and twin + (dg,) not in ordered:
-                    ordered.append(twin + (dg,))
-    near = [o for o in ordered if distance(o) <= reach]
-    far = [o for o in ordered if distance(o) > reach]
-    for o in far:
-        gaps = [tuple((p - q) % n for p, q, n in zip(o, m, sizes)) for m in middles]
-        assert any(distance(gap) <= reach for gap in gaps)
-    return near, far, [m for m in middles if m in near]
-
-
-def exchange(sizes, codes_hbm, exps_hbm, cmap_hbm, recv, codes, exps, cmap, turned, send, load_sem, send_sem, recv_sem, mid_sem):
+    ]
+
+    def distance(o):
+        return hops(o[0], x_size) + hops(o[1], y_size) + hops(o[2], z_size)
+
+    greeted = [o for o in offsets[1:] if o[:2] == (0, 0) or o[2] == 0]
+    greeted = sorted(greeted, key=lambda o: -distance(o))
+    column = [o for o in offsets[1:] if o[:2] == (0, 0)]
+    place = {
+        o + (0,): i / len(offsets)
+        + 0.07 * (o[0] >= x_size // 2) + 0.1 * (o[1] >= y_size // 2) + 0.3 * (o[2] >= z_size // 2)
+        for i, o in enumerate(offsets)
+    }
+    return greeted, column, sorted(place, key=lambda o: place[o])
+
+
+def exchange(sizes, codes_hbm, exps_hbm, cmap_hbm, recv, codes, exps, cmap, turned, send, load_sem, send_sem, recv_sem, line_sem):
     x_size, y_size, z_size, g_size = sizes
     devices = x_size * y_size * z_size * g_size
     layers, rows, width = codes.shape
     col_width = width // devices
-    near, far, middles = plan(sizes)
+    greeted, column, rest = plan(sizes)
+
+    chain, g = lax.axis_index("chain"), lax.axis_index("grp")
+    x, z = lax.rem(chain, x_size), lax.rem(lax.div(chain, x_size), z_size)
+    y = lax.div(chain, x_size * z_size)
+    me = chain * g_size + g
+    cores = [lax.rem(g + d, g_size) for d in range(g_size)]
+
+    def relative(at, size, step):
+        return [lax.rem(at + d, size) * step for d in range(size)]
+
+    def halved(at, size, step):
+        half = size // 2
+        turn = lax.rem(at, half)
+        return [(h * half + lax.rem(turn + i, half)) * step for h in range(2) for i in range(half)]
+
+    steps = ((x, x_size, 1), (y, y_size, x_size * z_size), (z, z_size, x_size))
+    near_x, near_y, near_z = (relative(*s) for s in steps)
+    all_x, all_y, all_z = (halved(*s) for s in steps)
+
+    def peer(o):
+        if len(o) == 4:
+            return near_y[o[1]] + near_x[o[0]] + near_z[o[2]], cores[o[3]]
+        return all_y[o[1]] + all_x[o[0]] + all_z[o[2]], cores[o[3]]
+
+    barrier = pltpu.get_barrier_semaphore()
+    for o in greeted:
+        pl.semaphore_signal(barrier, inc=1, device_id=peer(o), device_id_type=MESH)
 
     pieces = 2
     piece = width // pieces
@@ -65,22 +85,6 @@
         loads[-1].start()
     load_cmap = pltpu.make_async_copy(cmap_hbm, cmap, load_sem.at[pieces + 1])
     load_cmap.start()
-
-    chain, g = lax.axis_index("chain"), lax.axis_index("grp")
-    x, z, y = lax.rem(chain, x_size), lax.rem(lax.div(chain, x_size), z_size), lax.div(chain, x_size * z_size)
-    me = chain * g_size + g
-    across = [lax.rem(x + d, x_size) for d in range(x_size)]
-    along = [lax.rem(z + d, z_size) * x_size for d in range(z_size)]
-    down = [lax.rem(y + d, y_size) * (x_size * z_size) for d in range(y_size)]
-    cores = [lax.rem(g + d, g_size) for d in range(g_size)]
-    planes = {(dx, dy): down[dy] + across[dx] for dx in range(x_size) for dy in range(y_size)}
-
-    def peer(o):
-        return planes[o[:2]] + along[o[2]], cores[o[3]]
-
-    barrier = pltpu.get_barrier_semaphore()
-    for o in near:
-        pl.semaphore_signal(barrier, inc=1, device_id=peer(o), device_id_type=MESH)
 
     load_exps.wait()
     group = LANES // 8
@@ -103,31 +107,34 @@
         to, to_g = peer(o)
         send[slot] = turned[cmap[to * g_size + to_g]]
 
-    def launch(slot, o):
-        pltpu.make_async_remote_copy(
+    def copy(slot, o):
+        return pltpu.make_async_remote_copy(
             src_ref=send.at[slot],
             dst_ref=recv.at[me],
             send_sem=send_sem,
             recv_sem=recv_sem,
             device_id=peer(o),
             device_id_type=MESH,
-        ).start()
+        )
 
     recv[me] = turned[cmap[me]]
-    for slot, o in enumerate(near + far):
+    for slot, o in enumerate(column + rest):
         gather(slot, o)
 
-    pl.semaphore_wait(barrier, len(near))
-    for m in middles:
-        pl.semaphore_signal(mid_sem, inc=1, device_id=peer(m), device_id_type=MESH)
-    for slot, o in enumerate(near):
-        launch(slot, o)
-    pl.semaphore_wait(mid_sem, len(middles))
-    for slot, o in enumerate(far):
-        launch(len(near) + slot, o)
+    pl.semaphore_wait(barrier, len(greeted))
+    line = [(0, 0, d, 0) for d in range(1, z_size)]
+    for o in sorted(line, key=lambda o: -hops(o[2], z_size)):
+        pl.semaphore_signal(line_sem, inc=1, device_id=peer(o), device_id_type=MESH)
+    for slot, o in enumerate(column):
+        copy(slot, o).start()
+    pl.semaphore_wait(line_sem, len(line))
+    for slot, o in enumerate(rest):
+        here = (all_x[o[0]] == x).astype(jnp.int32) + (all_y[o[1]] == near_y[0]).astype(jnp.int32)
+        pl.when(here < 2)(copy(len(column) + slot, o).start)
+
     others = recv.at[pl.ds(0, devices - 1)]
     pltpu.make_async_copy(others, others, recv_sem).wait()
-    pltpu.make_async_copy(send, send, send_sem).wait()
+    pltpu.make_async_copy(others, others, send_sem).wait()
 
 
 def assemble(order, recv, rollout, sums, tiles, totals, out_sem):
@@ -173,6 +180,7 @@
 def shards(sizes, codes, exponents, column_map, row_order):
     layers, rows, width = codes.shape
     devices = sizes[0] * sizes[1] * sizes[2] * sizes[3]
+    column = sizes[2] * sizes[3]
     col_width = width // devices
     anywhere = pl.BlockSpec(memory_space=pl.ANY)
     landed = pl.pallas_call(
@@ -185,7 +193,7 @@
             pltpu.VMEM(exponents.shape, exponents.dtype),
             pltpu.SMEM(column_map.shape, column_map.dtype),
             pltpu.VMEM((devices, col_width, layers * rows), codes.dtype),
-            pltpu.VMEM((devices - 1, col_width, layers * rows), jnp.bfloat16),
+            pltpu.VMEM((devices + column - 1, col_width, layers * rows), jnp.bfloat16),
             pltpu.SemaphoreType.DMA((4,)),
             pltpu.SemaphoreType.DMA(()),
             pltpu.SemaphoreType.DMA(()),

time: 52.8 us -> 49.1 us (0.930)
  the two profiles are of different devices: /device:TPU:1 before, /device:TPU:49 now
where the time goes in v4:
time: 49.1 us; the launch traced here: 49 us
  Pallas kernels  48.3 us (98%)
  between operations  0.65 us (1%)
    pallas_call x1, Pallas kernels, shards(): pl.pallas_call(functools.partial(exchange, sizes), out_shape=pltpu.VMEM((...  46.1 us
    pallas_call x1, Pallas kernels, shards(): pl.pallas_call(assemble, out_shape=(rollout, sums), in_specs=[pl.BlockSpe...  2.17 us

profile of v4, /device:TPU:49, one launch (start us, length us, event | category | flops | bytes accessed | tf_op | source)
XLA Modules:
  0.0 49.0 jit_solution(6892197466016609008)
XLA Ops:
  0.6 0.0 copy-start
  0.6 46.1 %exchange.1.recv = bf16[256,24,128]{2,1,0:T(8,128)(2,1)S(1)} custom-call(bf16[2,64,6144]{2,1,0:T(8,128)(2,1)} %codes_hbm.1, s32[2,2,6144]{2,1,0:T(2,128)} %exps_hbm.1, s32[256]{0:T(256)} %cmap_hbm.1), custom_call_target="tpu_custom_call" | custom-call | tf_op jit(solution)/shard_map/exchange/pallas_call | solution.py:186
  46.8 0.0 copy-done
  46.8 2.2 %assemble.1 = (bf16[2,24,16384]{2,1,0:T(8,128)(2,1)}, f32[2,24,512]{2,1,0:T(8,128)}) custom-call(s32[256]{0:T(256)S(1)} %copy-done, bf16[256,24,128]{2,1,0:T(8,128)(2,1)S(1)} %exchange.1.recv), custom_call_target="tpu_custom_call" | custom-call | tf_op jit(solution)/shard_map/assemble/pallas_call | solution.py:209
Async XLA Ops:
  0.6 46.2 %copy-start = (s32[256]{0:T(256)S(1)}, s32[256]{0:T(256)}, u32[]{:S(2)}) copy-start(s32[256]{0:T(256)} %order.1) | copy-start | bytes 3076

commit v5 on v4

--- a/solution.py
+++ b/solution.py
@@ -32,15 +32,16 @@
     greeted = [o for o in offsets[1:] if o[:2] == (0, 0) or o[2] == 0]
     greeted = sorted(greeted, key=lambda o: -distance(o))
     column = [o for o in offsets[1:] if o[:2] == (0, 0)]
+    base = sorted(offsets, key=lambda o: ([0,2,1,3][o[1]],o[0],o[3],o[2]))
     place = {
         o + (0,): i / len(offsets)
-        + 0.07 * (o[0] >= x_size // 2) + 0.1 * (o[1] >= y_size // 2) + 0.3 * (o[2] >= z_size // 2)
-        for i, o in enumerate(offsets)
+        + 0.07 * (o[0] >= x_size // 2) + 0.2 * (o[1] >= y_size // 2) + 0.3 * (o[2] >= z_size // 2)
+        for i, o in enumerate(base)
     }
     return greeted, column, sorted(place, key=lambda o: place[o])
 
 
-def exchange(sizes, codes_hbm, exps_hbm, cmap_hbm, recv, codes, exps, cmap, turned, send, load_sem, send_sem, recv_sem, line_sem):
+def exchange(sizes, codes_hbm, exps_hbm, cmap_hbm, order_hbm, tiles, codes, exps, cmap, order, turned, send, recv, load_sem, send_sem, recv_sem, line_sem):
     x_size, y_size, z_size, g_size = sizes
     devices = x_size * y_size * z_size * g_size
     layers, rows, width = codes.shape
@@ -85,6 +86,8 @@
         loads[-1].start()
     load_cmap = pltpu.make_async_copy(cmap_hbm, cmap, load_sem.at[pieces + 1])
     load_cmap.start()
+    load_order = pltpu.make_async_copy(order_hbm, order, load_sem.at[pieces + 2])
+    load_order.start()
 
     load_exps.wait()
     group = LANES // 8
@@ -102,6 +105,7 @@
         blocks = jnp.concatenate(parts, axis=0).T.reshape(group, col_width, layers * rows)
         turned[pl.ds(chunk * group, group)] = blocks
     load_cmap.wait()
+    load_order.wait()
 
     def gather(slot, o):
         to, to_g = peer(o)
@@ -134,32 +138,33 @@
 
     others = recv.at[pl.ds(0, devices - 1)]
     pltpu.make_async_copy(others, others, recv_sem).wait()
+    half = LANES // layers
+    low = lax.broadcasted_iota(jnp.int32, (col_width, LANES), 1) < half
+
+    @pl.loop(0, devices * half // LANES, unroll=32)
+    def _(i):
+        lanes = pl.ds(pl.multiple_of(i * LANES, LANES), LANES)
+        a, b = recv[order[2 * i]], recv[order[2 * i + 1]]
+        crossed = pltpu.roll(jnp.where(low, b, a), half, 1)
+        tiles[0, :, lanes] = jnp.where(low, a, crossed)
+        tiles[1, :, lanes] = jnp.where(low, crossed, b)
+
     pltpu.make_async_copy(others, others, send_sem).wait()
 
 
-def assemble(order, recv, rollout, sums, tiles, totals, out_sem):
+def assemble(tiles, rollout, sums, totals, out_sem):
     layers, col_width, width = rollout.shape
-    half = LANES // layers
     quad = 2 * LANES
     span = LANES * BLOCK
-    part = span // 2
+    copies = []
+    for i in range(width // span):
+        lanes = pl.ds(i * span, span)
+        copies.append(pltpu.make_async_copy(tiles.at[:, :, lanes], rollout.at[:, :, lanes], out_sem.at[i]))
+        copies[-1].start()
     lane = lax.broadcasted_iota(jnp.int32, (col_width, LANES), 1)
-    low = lane < half
     sources = lax.broadcasted_iota(jnp.int32, (quad, LANES), 0) // BLOCK
     targets = lax.broadcasted_iota(jnp.int32, (quad, LANES), 1) % (quad // BLOCK)
     picks = (sources == targets).astype(jnp.bfloat16)
-    copies = []
-    for at in range(0, width, LANES):
-        k = at // half
-        a, b = recv[order[k]], recv[order[k + 1]]
-        crossed = pltpu.roll(jnp.where(low, b, a), half, 1)
-        tiles[0, :, at : at + LANES] = jnp.where(low, a, crossed)
-        tiles[1, :, at : at + LANES] = jnp.where(low, crossed, b)
-        done = at + LANES
-        if done % part == 0:
-            lanes = pl.ds(done - part, part)
-            copies.append(pltpu.make_async_copy(tiles.at[:, :, lanes], rollout.at[:, :, lanes], out_sem.at[done // part - 1]))
-            copies[-1].start()
     for start in range(0, width, span):
         for layer in range(layers):
             stacked = jnp.concatenate(
@@ -171,7 +176,7 @@
             for i in range(1, span // quad):
                 total = jnp.where(lane // (quad // BLOCK) == i, got[i], total)
             totals[layer, :, start // BLOCK : start // BLOCK + LANES] = total
-    copies.append(pltpu.make_async_copy(totals, sums, out_sem.at[width // part]))
+    copies.append(pltpu.make_async_copy(totals, sums, out_sem.at[width // span]))
     copies[-1].start()
     for copy in copies:
         copy.wait()
@@ -183,18 +188,21 @@
     column = sizes[2] * sizes[3]
     col_width = width // devices
     anywhere = pl.BlockSpec(memory_space=pl.ANY)
-    landed = pl.pallas_call(
+    tiled = (layers, col_width, devices * rows)
+    tiles = pl.pallas_call(
         functools.partial(exchange, sizes),
-        out_shape=pltpu.VMEM((devices, col_width, layers * rows), jnp.bfloat16),
-        in_specs=[anywhere] * 3,
+        out_shape=pltpu.VMEM(tiled, jnp.bfloat16),
+        in_specs=[anywhere] * 4,
         out_specs=pl.BlockSpec(memory_space=pltpu.VMEM),
         scratch_shapes=[
             pltpu.VMEM(codes.shape, codes.dtype),
             pltpu.VMEM(exponents.shape, exponents.dtype),
             pltpu.SMEM(column_map.shape, column_map.dtype),
+            pltpu.SMEM(row_order.shape, row_order.dtype),
             pltpu.VMEM((devices, col_width, layers * rows), codes.dtype),
             pltpu.VMEM((devices + column - 1, col_width, layers * rows), jnp.bfloat16),
-            pltpu.SemaphoreType.DMA((4,)),
+            pltpu.VMEM((devices, col_width, layers * rows), jnp.bfloat16),
+            pltpu.SemaphoreType.DMA((5,)),
             pltpu.SemaphoreType.DMA(()),
             pltpu.SemaphoreType.DMA(()),
             pltpu.SemaphoreType.REGULAR,
@@ -203,25 +211,23 @@
             collective_id=0, has_side_effects=True, vmem_limit_bytes=60 << 20
         ),
         name="exchange",
-    )(codes, exponents, column_map)
-    rollout = jax.ShapeDtypeStruct((layers, col_width, devices * rows), jnp.bfloat16)
+    )(codes, exponents, column_map, row_order)
+    rollout = jax.ShapeDtypeStruct(tiled, jnp.bfloat16)
     sums = jax.ShapeDtypeStruct((layers, col_width, devices * rows // BLOCK), jnp.float32)
     return pl.pallas_call(
         assemble,
         out_shape=(rollout, sums),
         in_specs=[
-            pl.BlockSpec(memory_space=pltpu.SMEM),
             pl.BlockSpec(memory_space=pltpu.VMEM),
         ],
         out_specs=(anywhere, anywhere),
         scratch_shapes=[
-            pltpu.VMEM(rollout.shape, rollout.dtype),
             pltpu.VMEM(sums.shape, sums.dtype),
-            pltpu.SemaphoreType.DMA((9,)),
+            pltpu.SemaphoreType.DMA((5,)),
         ],
         compiler_params=pltpu.CompilerParams(vmem_limit_bytes=16 << 20),
         name="assemble",
-    )(row_order, landed)
+    )(tiles)
 
 
 def solution(mesh):

time: 49.1 us -> 48.7 us (level)
  the two profiles are of different devices: /device:TPU:49 before, /device:TPU:31 now
where the time goes in v5:
time: 48.7 us; the launch traced here: 48.6 us
  Pallas kernels  48 us (99%)
  between operations  0.64 us (1%)
    pallas_call x1, Pallas kernels, shards(): pl.pallas_call(functools.partial(exchange, sizes), out_shape=pltpu.VMEM(t...  46.7 us
    pallas_call x1, Pallas kernels, shards(): pl.pallas_call(assemble, out_shape=(rollout, sums), in_specs=[pl.BlockSpe...  1.27 us

profile of v5, /device:TPU:31, one launch (start us, length us, event | category | flops | bytes accessed | tf_op | source)
XLA Modules:
  0.0 48.6 jit_solution(11139921076081141732)
XLA Ops:
  0.6 46.7 %exchange.1.tiles = bf16[2,24,16384]{2,1,0:T(8,128)(2,1)S(1)} custom-call(bf16[2,64,6144]{2,1,0:T(8,128)(2,1)} %codes_hbm.1, s32[2,2,6144]{2,1,0:T(2,128)} %exps_hbm.1, s32[256]{0:T(256)} %cmap_hbm.1, s32[256]{0:T(256)} %order_hbm.1), custom_call_target="tpu_custom_call" | custom-call | tf_op jit(solution)/shard_map/exchange/pallas_call | solution.py:192
  47.4 1.3 %assemble.1 = (bf16[2,24,16384]{2,1,0:T(8,128)(2,1)}, f32[2,24,512]{2,1,0:T(8,128)}) custom-call(bf16[2,24,16384]{2,1,0:T(8,128)(2,1)S(1)} %exchange.1.tiles), custom_call_target="tpu_custom_call" | custom-call | tf_op jit(solution)/shard_map/assemble/pallas_call | solution.py:217

commit v6 on v5

--- a/solution.py
+++ b/solution.py
@@ -29,7 +29,8 @@
     def distance(o):
         return hops(o[0], x_size) + hops(o[1], y_size) + hops(o[2], z_size)
 
-    greeted = [o for o in offsets[1:] if o[:2] == (0, 0) or o[2] == 0]
+    side = [o for o in offsets if o[:2] in ((1, 0), (3, 0)) and o[2] in (3, 5)]
+    greeted = [o for o in offsets[1:] if o[:2] == (0, 0) or o[2] == 0] + side
     greeted = sorted(greeted, key=lambda o: -distance(o))
     column = [o for o in offsets[1:] if o[:2] == (0, 0)]
     base = sorted(offsets, key=lambda o: ([0,2,1,3][o[1]],o[0],o[3],o[2]))
@@ -38,7 +39,7 @@
         + 0.07 * (o[0] >= x_size // 2) + 0.2 * (o[1] >= y_size // 2) + 0.3 * (o[2] >= z_size // 2)
         for i, o in enumerate(base)
     }
-    return greeted, column, sorted(place, key=lambda o: place[o])
+    return greeted, column, side, sorted(place, key=lambda o: place[o])
 
 
 def exchange(sizes, codes_hbm, exps_hbm, cmap_hbm, order_hbm, tiles, codes, exps, cmap, order, turned, send, recv, load_sem, send_sem, recv_sem, line_sem):
@@ -46,7 +47,8 @@
     devices = x_size * y_size * z_size * g_size
     layers, rows, width = codes.shape
     col_width = width // devices
-    greeted, column, rest = plan(sizes)
+    greeted, column, side, rest = plan(sizes)
+    first = column + side
 
     chain, g = lax.axis_index("chain"), lax.axis_index("grp")
     x, z = lax.rem(chain, x_size), lax.rem(lax.div(chain, x_size), z_size)
@@ -122,19 +124,29 @@
         )
 
     recv[me] = turned[cmap[me]]
-    for slot, o in enumerate(column + rest):
+    for slot, o in enumerate(first + rest):
         gather(slot, o)
 
     pl.semaphore_wait(barrier, len(greeted))
     line = [(0, 0, d, 0) for d in range(1, z_size)]
     for o in sorted(line, key=lambda o: -hops(o[2], z_size)):
         pl.semaphore_signal(line_sem, inc=1, device_id=peer(o), device_id_type=MESH)
-    for slot, o in enumerate(column):
+    for slot, o in enumerate(first):
         copy(slot, o).start()
     pl.semaphore_wait(line_sem, len(line))
+    same_x, same_y = ([(at == near[0]).astype(jnp.int32) for at in every] for every, near in ((all_x, near_x), (all_y, near_y)))
+    side_columns = sorted({o[:2] for o in side})
+    side_depths = sorted({o[2] for o in side})
+    own, aside = {}, {}
+    for jx in range(x_size):
+        for jy in range(y_size):
+            own[jx, jy] = same_x[jx] * same_y[jy]
+            hits = [(all_x[jx] == near_x[dx]).astype(jnp.int32) * (all_y[jy] == near_y[dy]).astype(jnp.int32) for dx, dy in side_columns]
+            aside[jx, jy] = sum(hits)
+    deep = [sum((at == near_z[d]).astype(jnp.int32) for d in side_depths) for at in all_z]
     for slot, o in enumerate(rest):
-        here = (all_x[o[0]] == x).astype(jnp.int32) + (all_y[o[1]] == near_y[0]).astype(jnp.int32)
-        pl.when(here < 2)(copy(len(column) + slot, o).start)
+        sent = own[o[0], o[1]] + aside[o[0], o[1]] * deep[o[2]]
+        pl.when(sent == 0)(copy(len(first) + slot, o).start)
 
     others = recv.at[pl.ds(0, devices - 1)]
     pltpu.make_async_copy(others, others, recv_sem).wait()
@@ -185,7 +197,8 @@
 def shards(sizes, codes, exponents, column_map, row_order):
     layers, rows, width = codes.shape
     devices = sizes[0] * sizes[1] * sizes[2] * sizes[3]
-    column = sizes[2] * sizes[3]
+    greeted, column, side, rest = plan(sizes)
+    first = len(column + side)
     col_width = width // devices
     anywhere = pl.BlockSpec(memory_space=pl.ANY)
     tiled = (layers, col_width, devices * rows)
@@ -200,7 +213,7 @@
             pltpu.SMEM(column_map.shape, column_map.dtype),
             pltpu.SMEM(row_order.shape, row_order.dtype),
             pltpu.VMEM((devices, col_width, layers * rows), codes.dtype),
-            pltpu.VMEM((devices + column - 1, col_width, layers * rows), jnp.bfloat16),
+            pltpu.VMEM((devices + first, col_width, layers * rows), jnp.bfloat16),
             pltpu.VMEM((devices, col_width, layers * rows), jnp.bfloat16),
             pltpu.SemaphoreType.DMA((5,)),
             pltpu.SemaphoreType.DMA(()),

time: 48.7 us -> 48.7 us (level)
  no operation moved by 1% of the time
where the time goes in v6:
time: 48.7 us; the launch traced here: 48.6 us
  Pallas kernels  48 us (99%)
  between operations  0.64 us (1%)
    pallas_call x1, Pallas kernels, shards(): pl.pallas_call(functools.partial(exchange, sizes), out_shape=pltpu.VMEM(t...  46.7 us
    pallas_call x1, Pallas kernels, shards(): pl.pallas_call(assemble, out_shape=(rollout, sums), in_specs=[pl.BlockSpe...  1.27 us

profile of v6, /device:TPU:31, one launch (start us, length us, event | category | flops | bytes accessed | tf_op | source)
XLA Modules:
  0.0 48.6 jit_solution(3505795886394512747)
XLA Ops:
  0.6 46.7 %exchange.1.tiles = bf16[2,24,16384]{2,1,0:T(8,128)(2,1)S(1)} custom-call(bf16[2,64,6144]{2,1,0:T(8,128)(2,1)} %codes_hbm.1, s32[2,2,6144]{2,1,0:T(2,128)} %exps_hbm.1, s32[256]{0:T(256)} %cmap_hbm.1, s32[256]{0:T(256)} %order_hbm.1), custom_call_target="tpu_custom_call" | custom-call | tf_op jit(solution)/shard_map/exchange/pallas_call | solution.py:205
  47.4 1.3 %assemble.1 = (bf16[2,24,16384]{2,1,0:T(8,128)(2,1)}, f32[2,24,512]{2,1,0:T(8,128)}) custom-call(bf16[2,24,16384]{2,1,0:T(8,128)(2,1)S(1)} %exchange.1.tiles), custom_call_target="tpu_custom_call" | custom-call | tf_op jit(solution)/shard_map/assemble/pallas_call | solution.py:230

commit v7 on v6

--- a/solution.py
+++ b/solution.py
@@ -153,13 +153,17 @@
     half = LANES // layers
     low = lax.broadcasted_iota(jnp.int32, (col_width, LANES), 1) < half
 
-    @pl.loop(0, devices * half // LANES, unroll=32)
+    @pl.loop(0, devices * half // (4 * LANES), unroll=8)
     def _(i):
-        lanes = pl.ds(pl.multiple_of(i * LANES, LANES), LANES)
-        a, b = recv[order[2 * i]], recv[order[2 * i + 1]]
-        crossed = pltpu.roll(jnp.where(low, b, a), half, 1)
-        tiles[0, :, lanes] = jnp.where(low, a, crossed)
-        tiles[1, :, lanes] = jnp.where(low, crossed, b)
+        lanes = pl.ds(pl.multiple_of(i * 4 * LANES, 4 * LANES), 4 * LANES)
+        lows, highs = [], []
+        for j in range(4):
+            a, b = recv[order[8 * i + 2 * j]], recv[order[8 * i + 2 * j + 1]]
+            crossed = pltpu.roll(jnp.where(low, b, a), half, 1)
+            lows.append(jnp.where(low, a, crossed))
+            highs.append(jnp.where(low, crossed, b))
+        tiles[0, :, lanes] = jnp.concatenate(lows, axis=1)
+        tiles[1, :, lanes] = jnp.concatenate(highs, axis=1)
 
     pltpu.make_async_copy(others, others, send_sem).wait()
 

time: 48.7 us -> 48.7 us (level)
  no operation moved by 1% of the time
where the time goes in v7:
time: 48.7 us; the launch traced here: 48.6 us
  Pallas kernels  47.9 us (98%)
  between operations  0.64 us (1%)
    pallas_call x1, Pallas kernels, shards(): pl.pallas_call(functools.partial(exchange, sizes), out_shape=pltpu.VMEM(t...  46.7 us
    pallas_call x1, Pallas kernels, shards(): pl.pallas_call(assemble, out_shape=(rollout, sums), in_specs=[pl.BlockSpe...  1.27 us

profile of v7, /device:TPU:31, one launch (start us, length us, event | category | flops | bytes accessed | tf_op | source)
XLA Modules:
  0.0 48.6 jit_solution(6474929173437454540)
XLA Ops:
  0.6 46.7 %exchange.1.tiles = bf16[2,24,16384]{2,1,0:T(8,128)(2,1)S(1)} custom-call(bf16[2,64,6144]{2,1,0:T(8,128)(2,1)} %codes_hbm.1, s32[2,2,6144]{2,1,0:T(2,128)} %exps_hbm.1, s32[256]{0:T(256)} %cmap_hbm.1, s32[256]{0:T(256)} %order_hbm.1), custom_call_target="tpu_custom_call" | custom-call | tf_op jit(solution)/shard_map/exchange/pallas_call | solution.py:209
  47.3 1.3 %assemble.1 = (bf16[2,24,16384]{2,1,0:T(8,128)(2,1)}, f32[2,24,512]{2,1,0:T(8,128)}) custom-call(bf16[2,24,16384]{2,1,0:T(8,128)(2,1)S(1)} %exchange.1.tiles), custom_call_target="tpu_custom_call" | custom-call | tf_op jit(solution)/shard_map/assemble/pallas_call | solution.py:234
